TPU v7x, 32 devices: a whole 2x2x4 slice. The times are simulated.
32 devices in a mesh: fsdp: 32 (over z, y, x, core).
Axes of the slice: x: 2, y: 2, z: 4, core: 2. Of those that a mesh axis runs over, the one named last changes fastest.
Arguments:
- tok_ids: int32 [32, 256], P('fsdp')
- grad_out: bfloat16 [32, 256, 2048], P('fsdp')
- emb_table: bfloat16 [151936, 2048], P('fsdp')
- norm_gain: bfloat16 [2048], P('fsdp')
- w_query: bfloat16 [2048, 2048], P('fsdp')
- b_query: bfloat16 [2048], P('fsdp')
- w_key: bfloat16 [2048, 256], P('fsdp')
- b_key: bfloat16 [256], P('fsdp')
- w_value: bfloat16 [2048, 256], P('fsdp')
- b_value: bfloat16 [256], P('fsdp')
- w_out: bfloat16 [2048, 2048], P('fsdp')
Outputs:
- output 1: bfloat16 [32, 256, 2048], P('fsdp')
- output 2: bfloat16 [151936, 2048], P('fsdp')
- output 3: float32 [2048], P('fsdp')
- output 4: float32 [2048, 2048], P('fsdp')
- output 5: float32 [2048], P('fsdp')
- output 6: float32 [2048, 256], P('fsdp')
- output 7: float32 [256], P('fsdp')
- output 8: float32 [2048, 256], P('fsdp')
- output 9: float32 [256], P('fsdp')
- output 10: float32 [2048, 2048], P('fsdp')
All inputs are finite; a program needn't handle non-finite values.
Results may differ from a plain program's by a relative error of at most 0.0179842.
Values are sent between devices in bfloat16 or wider.
A program may use at most 1 GiB of HBM per device.

v0:
```python
import jax
import jax.numpy as jnp
from jax import lax
from jax.sharding import PartitionSpec as P

HEAD_DIM = 128
ROPE_THETA = 1.0e6
NORM_EPS = 1e-6
MASK_VALUE = -1e30


def rope_tables(seq_len):
    half_dim = HEAD_DIM // 2
    inv_freq = jnp.power(ROPE_THETA, -(jnp.arange(half_dim, dtype=jnp.float32) * 2.0 / HEAD_DIM))
    angles = jnp.arange(seq_len, dtype=jnp.float32)[:, None] * inv_freq[None, :]
    angles = jnp.concatenate([angles, angles], axis=-1)
    return jnp.cos(angles)[:, None, :], jnp.sin(angles)[:, None, :]


def rotate(vector, cos_t, sin_t):
    half_dim = HEAD_DIM // 2
    turned = jnp.concatenate([-vector[..., half_dim:], vector[..., :half_dim]], axis=-1)
    return vector * cos_t + turned * sin_t


def rotate_back(grad_in, cos_t, sin_t):
    half_dim = HEAD_DIM // 2
    scaled = grad_in * sin_t
    turned = jnp.concatenate([scaled[..., half_dim:], -scaled[..., :half_dim]], axis=-1)
    return grad_in * cos_t + turned


def block_fwd_bwd(x_rows, grad_out, gain_vec, w_query, b_query, w_key, b_key, w_value, b_value, w_out):
    batch_size, seq_len, model_width = x_rows.shape
    n_heads = w_query.shape[1] // HEAD_DIM
    kv_heads = w_key.shape[1] // HEAD_DIM
    q_group = n_heads // kv_heads
    score_scale = HEAD_DIM ** -0.5
    cos_t, sin_t = rope_tables(seq_len)
    x_full = x_rows.astype(jnp.float32)
    inv_rms = lax.rsqrt(jnp.mean(x_full * x_full, axis=-1, keepdims=True) + NORM_EPS)
    x_norm = x_full * inv_rms
    gain_f = gain_vec.astype(jnp.float32)
    hidden = (x_norm * gain_f).astype(jnp.bfloat16)
    q_lin = jnp.einsum("bli,io->blo", hidden, w_query, preferred_element_type=jnp.float32) + b_query.astype(jnp.float32)
    k_lin = jnp.einsum("bli,io->blo", hidden, w_key, preferred_element_type=jnp.float32) + b_key.astype(jnp.float32)
    v_lin = jnp.einsum("bli,io->blo", hidden, w_value, preferred_element_type=jnp.float32) + b_value.astype(jnp.float32)
    q_rot = rotate(q_lin.reshape(batch_size, seq_len, n_heads, HEAD_DIM), cos_t, sin_t).astype(jnp.bfloat16)
    q_rot = q_rot.reshape(batch_size, seq_len, kv_heads, q_group, HEAD_DIM)
    k_rot = rotate(k_lin.reshape(batch_size, seq_len, kv_heads, HEAD_DIM), cos_t, sin_t).astype(jnp.bfloat16)
    v_val = v_lin.astype(jnp.bfloat16).reshape(batch_size, seq_len, kv_heads, HEAD_DIM)
    scores = jnp.einsum("bqkgd,bskd->bkgqs", q_rot, k_rot, preferred_element_type=jnp.float32) * score_scale
    causal = jnp.arange(seq_len)[:, None] >= jnp.arange(seq_len)[None, :]
    scores = jnp.where(causal, scores, MASK_VALUE)
    prob_f = jax.nn.softmax(scores, axis=-1)
    prob_b = prob_f.astype(jnp.bfloat16)
    attn_out = jnp.einsum("bkgqs,bskd->bqkgd", prob_b, v_val, preferred_element_type=jnp.float32)
    attn_b = attn_out.astype(jnp.bfloat16).reshape(batch_size, seq_len, n_heads * HEAD_DIM)
    proj_out = jnp.einsum("bli,io->blo", attn_b, w_out, preferred_element_type=jnp.float32)
    block_out = (x_full + proj_out).astype(jnp.bfloat16)

    grad_wo = jnp.einsum("bli,blo->io", attn_b, grad_out, preferred_element_type=jnp.float32)
    d_attn = jnp.einsum("blo,io->bli", grad_out, w_out, preferred_element_type=jnp.float32)
    d_attn = d_attn.astype(jnp.bfloat16).reshape(batch_size, seq_len, kv_heads, q_group, HEAD_DIM)
    d_probs = jnp.einsum("bqkgd,bskd->bkgqs", d_attn, v_val, preferred_element_type=jnp.float32)
    d_val = jnp.einsum("bkgqs,bqkgd->bskd", prob_b, d_attn, preferred_element_type=jnp.float32)
    d_scores = prob_f * (d_probs - jnp.sum(d_probs * prob_f, axis=-1, keepdims=True))
    d_scores = (d_scores * score_scale).astype(jnp.bfloat16)
    d_qrot = jnp.einsum("bkgqs,bskd->bqkgd", d_scores, k_rot, preferred_element_type=jnp.float32)
    d_krot = jnp.einsum("bkgqs,bqkgd->bskd", d_scores, q_rot, preferred_element_type=jnp.float32)
    d_query = rotate_back(d_qrot.reshape(batch_size, seq_len, n_heads, HEAD_DIM), cos_t, sin_t)
    d_query = d_query.reshape(batch_size, seq_len, n_heads * HEAD_DIM)
    d_key = rotate_back(d_krot, cos_t, sin_t).reshape(batch_size, seq_len, kv_heads * HEAD_DIM)
    d_value = d_val.reshape(batch_size, seq_len, kv_heads * HEAD_DIM)
    grad_bq = jnp.sum(d_query, axis=(0, 1))
    grad_bk = jnp.sum(d_key, axis=(0, 1))
    grad_bv = jnp.sum(d_value, axis=(0, 1))
    dq_b = d_query.astype(jnp.bfloat16)
    dk_b = d_key.astype(jnp.bfloat16)
    dv_b = d_value.astype(jnp.bfloat16)
    grad_wq = jnp.einsum("bli,blo->io", hidden, dq_b, preferred_element_type=jnp.float32)
    grad_wk = jnp.einsum("bli,blo->io", hidden, dk_b, preferred_element_type=jnp.float32)
    grad_wv = jnp.einsum("bli,blo->io", hidden, dv_b, preferred_element_type=jnp.float32)
    d_hidden = jnp.einsum("blo,io->bli", dq_b, w_query, preferred_element_type=jnp.float32)
    d_hidden = d_hidden + jnp.einsum("blo,io->bli", dk_b, w_key, preferred_element_type=jnp.float32)
    d_hidden = d_hidden + jnp.einsum("blo,io->bli", dv_b, w_value, preferred_element_type=jnp.float32)
    grad_gain = jnp.sum(d_hidden * x_norm, axis=(0, 1))
    d_norm = d_hidden * gain_f
    d_x = grad_out.astype(jnp.float32) + inv_rms * (d_norm - x_norm * jnp.mean(d_norm * x_norm, axis=-1, keepdims=True))
    return block_out, d_x, (grad_gain, grad_wq, grad_bq, grad_wk, grad_bk, grad_wv, grad_bv, grad_wo)


def solution(mesh):
    row_spec = P("fsdp", None)
    vec_spec = P("fsdp")
    act_spec = P("fsdp", None, None)
    weight_specs = (vec_spec, row_spec, vec_spec, row_spec, vec_spec, row_spec, vec_spec, row_spec)
    in_specs = (row_spec, act_spec, row_spec) + weight_specs
    out_specs = (act_spec, row_spec) + weight_specs

    def device_step(tok_ids, grad_out, table_part, gain_part, wq_part, bq_part, wk_part, bk_part, wv_part, bv_part, wo_part):
        rows_dev = table_part.shape[0]
        model_width = table_part.shape[1]
        first_row = lax.axis_index("fsdp") * rows_dev
        all_ids = lax.all_gather(tok_ids, "fsdp")
        local_idx = all_ids - first_row
        is_owned = (local_idx >= 0) & (local_idx < rows_dev)
        looked = jnp.take(table_part, jnp.where(is_owned, local_idx, 0), axis=0)
        looked = jnp.where(is_owned[..., None], looked, jnp.zeros((), jnp.bfloat16))
        x_rows = lax.psum_scatter(looked, "fsdp", scatter_dimension=0)
        gain_full = lax.all_gather(gain_part, "fsdp", axis=0, tiled=True)
        wq_full = lax.all_gather(wq_part, "fsdp", axis=0, tiled=True)
        bq_full = lax.all_gather(bq_part, "fsdp", axis=0, tiled=True)
        wk_full = lax.all_gather(wk_part, "fsdp", axis=0, tiled=True)
        bk_full = lax.all_gather(bk_part, "fsdp", axis=0, tiled=True)
        wv_full = lax.all_gather(wv_part, "fsdp", axis=0, tiled=True)
        bv_full = lax.all_gather(bv_part, "fsdp", axis=0, tiled=True)
        wo_full = lax.all_gather(wo_part, "fsdp", axis=0, tiled=True)
        block_out, d_x, grad_list = block_fwd_bwd(x_rows, grad_out, gain_full, wq_full, bq_full, wk_full, bk_full, wv_full, bv_full, wo_full)
        all_dx = lax.all_gather(d_x, "fsdp")
        seg_idx = jnp.where(is_owned, local_idx, rows_dev)
        grad_part = jax.ops.segment_sum(all_dx.reshape(-1, model_width), seg_idx.reshape(-1), num_segments=rows_dev)
        reduced = tuple(lax.psum_scatter(grad_full, "fsdp", scatter_dimension=0, tiled=True) for grad_full in grad_list)
        return (block_out, grad_part.astype(jnp.bfloat16)) + reduced

    return jax.shard_map(device_step, mesh=mesh, in_specs=in_specs, out_specs=out_specs, check_vma=False)
```

profile of v0, /device:TPU:0, one launch (start us, length us, event | category | flops | bytes accessed | tf_op | source)
XLA Modules:
  0.0 1733.5 jit_solution(4343500487127085124)
XLA Ops:
  8.0 43.5 %all-gather.2 = s32[32,1,256]{2,1,0:T(1,128)S(1)} all-gather(s32[1,1,256]{2,1,0:T(1,128)} %bitcast.231), channel_id=2, replica_groups=mesh['fsdp'=32] {'fsdp'}, dimensions={0}, use_global_device_ids=true | all-gather | bytes 33792 | tf_op jit(solution)/shard_map/all_gather | solution.py:105
  52.1 70.4 %gather_fusion = bf16[8192,2048]{1,0:T(8,128)(2,1)} fusion(bf16[4748,2048]{1,0:T(8,128)(2,1)} %param.13, s32[8192]{0:T(1024)S(1)} %broadcast_clamp_fusion), kind=kCustom, calls=%fused_computation | custom fusion | bytes 67141632 | tf_op jit(solution)/shard_map/jit(_take)/gather | solution.py:108
  122.5 22.9 %select_select_fusion = bf16[32,1,256,2048]{3,2,1,0:T(8,128)(2,1)} fusion(bf16[32,1,256,2048]{3,2,1,0:T(8,128)(2,1)} %bitcast.206, pred[32,256]{1,0:T(8,128)(4,1)S(1)} %get-tuple-element.41, pred[32,256]{1,0:T(8,128)(4,1)S(1)} %get-tuple-element.40), kind=kLoop, calls=%fused_computation.2 | loop fusion | flops 33554432 | bytes 67125248 | tf_op jit(solution)/shard_map/jit(_where)/select_n | solution.py:109
  148.5 59.5 %all-reduce.9 = (bf16[256]{0:T(256)(128)(2,1)S(1)}, bf16[2048]{0:T(1024)(128)(2,1)S(1)}, bf16[256]{0:T(256)(128)(2,1)S(1)}, bf16[2048]{0:T(1024)(128)(2,1)S(1)}) all-reduce(bf16[256]{0:T(256)(128)(2,1)S(1)} %dynamic-update-slice.1, bf16[2048]{0:T(1024)(128)(2,1)S(1)} %dynamic-update-slice, ...), channel_id=1, replica_groups=mesh['fsdp'=32] {'fsdp'}, use_global_device_ids=true, to_apply=%add.1 | all-reduce | flops 4608 | bytes 18432
  209.2 5.7 fusion.35
  216.1 281.3 %reduce-scatter.6.cloned.1.call-done = bf16[1,1,256,2048]{3,2,1,0:T(8,128)(2,1)} async-done(((bf16[32,1,256,2048]{3,2,1,0:T(8,128)(2,1)}), bf16[1,1,256,2048]{3,2,1,0:T(8,128)(2,1)}) %reduce-scatter.6.cloned.1.call-update) | async-done | bytes 1048592 | tf_op jit(solution)/shard_map/reduce_scatter | solution.py:110
  499.0 85.3 %all-gather.13.cloned.1.call-done = bf16[2048,2048]{1,0:T(8,128)(2,1)} async-done(((bf16[64,2048]{1,0:T(8,128)(2,1)}), bf16[2048,2048]{1,0:T(8,128)(2,1)}) %all-gather.13.cloned.1.call-update) | async-done | bytes 8388624 | tf_op jit(solution)/shard_map/all_gather | solution.py:112
  584.2 7.4 convolution_add_fusion.2
  591.7 2.6 copy.90
  594.3 45.2 %all-gather.11.cloned.1.call-done = bf16[2048,256]{1,0:T(8,128)(2,1)} async-done(((bf16[64,256]{1,0:T(8,128)(2,1)}), bf16[2048,256]{1,0:T(8,128)(2,1)}) %all-gather.11.cloned.1.call-update) | async-done | bytes 1048592 | tf_op jit(solution)/shard_map/all_gather | solution.py:114
  646.0 48.7 %all-gather.9.cloned.1.call-done = bf16[2048,256]{1,0:T(8,128)(2,1)} async-done(((bf16[64,256]{1,0:T(8,128)(2,1)}), bf16[2048,256]{1,0:T(8,128)(2,1)}) %all-gather.9.cloned.1.call-update) | async-done | bytes 1048592 | tf_op jit(solution)/shard_map/all_gather | solution.py:116
  696.6 3.9 fusion.2
  700.6 2.8 fusion.27
  706.1 4.7 copy.78
  729.8 9.4 fusion.57
  743.3 8.1 fusion.38
  754.1 41.5 %all-reduce.8 = (f32[2048]{0:T(1024)S(1)}, f32[2048]{0:T(1024)S(1)}, f32[256]{0:T(256)S(1)}, f32[256]{0:T(256)S(1)}) all-reduce(f32[2048]{0:T(1024)S(1)} %copy-done.22, f32[2048]{0:T(1024)S(1)} %bitcast.227, f32[256]{0:T(256)S(1)} %bitcast.230, f32[256]{0:T(256)S(1)} %bitcast.229), channel_id=5, replica_groups=mesh['fsdp'=32] {'fsdp'}, use_global_device_ids=true, to_apply=%region_8.9.clone | all-reduce | flops 4608 | bytes 36864
  798.0 7.0 fusion.16
  805.0 276.2 %all-gather.17.cloned.1.call-done = f32[32,256,2048]{2,1,0:T(8,128)} async-done(((f32[1,256,2048]{2,1,0:T(8,128)}), f32[32,256,2048]{2,1,0:T(8,128)}) %all-gather.17.cloned.1.call-update) | async-done | bytes 67108880 | tf_op jit(solution)/shard_map/all_gather | solution.py:120
  1081.2 117.3 %scatter_custom_fusion = f32[4748,2048]{1,0:T(8,128)} fusion(s32[8192]{0:T(1024)S(1)} %bitcast.228, f32[8192,2048]{1,0:T(8,128)} %bitcast.50, f32[]{:T(128)} %constant.20.clone.1), kind=kCustom, calls=%fused_computation.3 | custom fusion | flops 16777216 | bytes 38896128 | tf_op jit(solution)/shard_map/scatter-add | solution.py:122
  1198.6 21.1 %convert_element_type.184 = bf16[4748,2048]{1,0:T(8,128)(2,1)} convert(f32[4748,2048]{1,0:T(8,128)} %scatter_custom_fusion) | non-fusion elementwise | flops 9723904 | bytes 58343424 | tf_op jit(solution)/shard_map/convert_element_type | solution.py:124
  1221.0 136.7 %reduce-scatter.10.cloned.1.call-done = f32[64,256]{1,0:T(8,128)} async-done(((f32[2048,256]{1,0:T(8,128)}), f32[64,256]{1,0:T(8,128)}) %reduce-scatter.10.cloned.1.call-update) | async-done | bytes 65552 | tf_op jit(solution)/shard_map/reduce_scatter | solution.py:123
  1357.7 181.5 %reduce-scatter.8.cloned.1.call-done = f32[64,2048]{1,0:T(8,128)} async-done(((f32[2048,2048]{1,0:T(8,128)}), f32[64,2048]{1,0:T(8,128)}) %reduce-scatter.8.cloned.1.call-update) | async-done | bytes 524304 | tf_op jit(solution)/shard_map/reduce_scatter | solution.py:123
  1539.2 187.3 %reduce-scatter.14.cloned.1.call-done = f32[64,2048]{1,0:T(8,128)} async-done(((f32[2048,2048]{1,0:T(8,128)}), f32[64,2048]{1,0:T(8,128)}) %reduce-scatter.14.cloned.1.call-update) | async-done | bytes 524304 | tf_op jit(solution)/shard_map/reduce_scatter | solution.py:123
  (139 shorter events, 48.4 us)
Async XLA Ops:
  7.2 202.0 %all-gather.15.cloned.1.call-start = ((), (), s32[]{:S(2)}) async-start(), calls=%async_computation.9 | async-start | bytes 8650752 | tf_op jit(solution)/shard_map/all_gather | solution.py:118
  7.9 489.5 %reduce-scatter.6.cloned.1.call-start = ((), (), s32[]{:S(2)}) async-start(), calls=%async_computation.5 | async-start | bytes 34603008 | tf_op jit(solution)/shard_map/reduce_scatter | solution.py:110
  145.4 2.3 copy-start.25
  145.4 2.6 copy-start.26
  145.4 2.8 copy-start.27
  145.4 63.7 %copy-start.8 = (bf16[1,256,2048]{2,1,0:T(8,128)(2,1)S(1)}, bf16[1,256,2048]{2,1,0:T(8,128)(2,1)}, u32[]{:S(2)}) copy-start(bf16[1,256,2048]{2,1,0:T(8,128)(2,1)} %param.12) | copy-start | bytes 3145732
  145.4 438.8 %all-gather.13.cloned.1.call-start = ((), (), s32[]{:S(2)}) async-start(), calls=%async_computation.8 | async-start | bytes 8650752 | tf_op jit(solution)/shard_map/all_gather | solution.py:112
  146.2 493.3 %all-gather.11.cloned.1.call-start = ((), (), s32[]{:S(2)}) async-start(), calls=%async_computation.7 | async-start | bytes 1081344 | tf_op jit(solution)/shard_map/all_gather | solution.py:114
  146.8 547.9 %all-gather.9.cloned.1.call-start = ((), (), s32[]{:S(2)}) async-start(), calls=%async_computation.6 | async-start | bytes 1081344 | tf_op jit(solution)/shard_map/all_gather | solution.py:116
  147.3 933.9 %all-gather.17.cloned.1.call-start = ((), (), s32[]{:S(2)}) async-start(), calls=%async_computation.14 | async-start | bytes 69206016 | tf_op jit(solution)/shard_map/all_gather | solution.py:120
  591.7 47.8 %copy-start = (bf16[1,1,256,2048]{3,2,1,0:T(8,128)(2,1)S(1)}, bf16[1,1,256,2048]{3,2,1,0:T(8,128)(2,1)}, u32[]{:S(2)}) copy-start(bf16[1,1,256,2048]{3,2,1,0:T(8,128)(2,1)} %reduce-scatter.6.cloned.1.call-done) | copy-start | bytes 3145732
  591.7 47.8 %copy-start.28 = (f32[256]{0:T(256)S(1)}, f32[256]{0:T(256)}, u32[]{:S(2)}) copy-start(f32[256]{0:T(256)} %convert_element_type.166) | copy-start | bytes 3076
  646.0 50.6 %copy-start.11 = (bf16[32,8,16,128]{3,2,1,0:T(8,128)(2,1)S(1)}, bf16[32,8,16,128]{3,2,1,0:T(8,128)(2,1)}, u32[]{:S(2)}) copy-start(bf16[32,8,16,128]{3,2,1,0:T(8,128)(2,1)} %copy.95) | copy-start | bytes 3145732
  696.6 4.0 copy-start.19
  696.6 3.9 copy-start.2
  700.6 2.9 copy-start.7
  713.6 4.4 slice-start
  713.8 4.6 slice-start.1
  718.4 2.4 copy-start.14
  725.7 495.3 %reduce-scatter.12.cloned.1.call-start = ((), (), s32[]{:S(2)}) async-start(), calls=%async_computation.12 | async-start | bytes 2162688 | tf_op jit(solution)/shard_map/reduce_scatter | solution.py:123
  727.8 629.9 %reduce-scatter.10.cloned.1.call-start = ((), (), s32[]{:S(2)}) async-start(), calls=%async_computation.11 | async-start | bytes 2162688 | tf_op jit(solution)/shard_map/reduce_scatter | solution.py:123
  729.8 809.4 %reduce-scatter.8.cloned.1.call-start = ((), (), s32[]{:S(2)}) async-start(), calls=%async_computation.10 | async-start | bytes 17301504 | tf_op jit(solution)/shard_map/reduce_scatter | solution.py:123
  739.3 987.1 %reduce-scatter.14.cloned.1.call-start = ((), (), s32[]{:S(2)}) async-start(), calls=%async_computation.13 | async-start | bytes 17301504 | tf_op jit(solution)/shard_map/reduce_scatter | solution.py:123
  740.2 3.1 copy-start.10
  (17 other events, 25.2 us)
Sparse Core Ops, SparseCore 0:
  10.8 79.6 all-gather.14
  145.6 351.8 reduce-scatter.5
  500.3 83.8 all-gather.12
  587.0 52.4 all-gather.10
  642.2 52.4 all-gather.8
  725.8 355.3 all-gather.16
  1084.0 136.8 reduce-scatter.11
  1223.8 133.8 reduce-scatter.9
  1360.5 178.5 reduce-scatter.7
  1541.9 184.4 reduce-scatter.13
where the time goes:
time: 1740 us; the launch traced here: 1730 us
  waiting for transfers between devices  1250 us (72%)
  other arithmetic  177 us (10%)
  blocking collectives  144 us (8%)
  local copies, waits for them, and re-layouts  89.8 us (5%)
  matrix products  61.4 us (4%)
    reduce_scatter x4, waiting for transfers between devices, device_step(): lax.psum_scatter(grad_full, 'fsdp', scatter_dimension=0, tiled=True)  507 us
    reduce_scatter x1, waiting for transfers between devices, device_step(): x_rows = lax.psum_scatter(looked, 'fsdp', scatter_dimension=0)  281 us
    all_gather x1, waiting for transfers between devices, device_step(): all_dx = lax.all_gather(d_x, 'fsdp')  276 us
    scatter-add x1, other arithmetic, device_step(): jax.ops.segment_sum(all_dx.reshape(-1, model_width), seg_idx.reshape(-1),...  117 us
    unnamed x2, blocking collectives  101 us
    all_gather x1, waiting for transfers between devices, device_step(): wq_full = lax.all_gather(wq_part, 'fsdp', axis=0, tiled=True)  85.3 us
    gather x1, local copies, waits for them, and re-layouts, device_step(): looked = jnp.take(table_part, jnp.where(is_owned, local_idx, 0), axis=0)  70.4 us
    all_gather x1, waiting for transfers between devices, device_step(): wv_full = lax.all_gather(wv_part, 'fsdp', axis=0, tiled=True)  48.7 us
  transfers between devices with their start and end apart: 10, of which 9 were waited for; matrix products, arithmetic and copies ran while one was open for 17% of the time, Pallas kernels for 0%

commit v1 on v0

v1 whole, which is shorter than its diff:
```python
import functools

import jax
import jax.numpy as jnp
from jax import lax
from jax.experimental import pallas as pl
from jax.experimental.pallas import tpu as pltpu
from jax.sharding import PartitionSpec as P

HEAD_DIM = 128
ROPE_THETA = 1.0e6
NORM_EPS = 1e-6
MASK_VALUE = -1e30
N_DEV = 32
HOT_CAP = 176
COLD_CAP = 16
QKV = 2560
WCOLS = 4608
MESH = pl.DeviceIdType.MESH


def rope_tables(seq_len):
    half_dim = HEAD_DIM // 2
    inv_freq = jnp.power(ROPE_THETA, -(jnp.arange(half_dim, dtype=jnp.float32) * 2.0 / HEAD_DIM))
    angles = jnp.arange(seq_len, dtype=jnp.float32)[:, None] * inv_freq[None, :]
    angles = jnp.concatenate([angles, angles], axis=-1)
    return jnp.cos(angles)[:, None, :], jnp.sin(angles)[:, None, :]


def rotate(vector, cos_t, sin_t):
    half_dim = HEAD_DIM // 2
    turned = jnp.concatenate([-vector[..., half_dim:], vector[..., :half_dim]], axis=-1)
    return vector * cos_t + turned * sin_t


def rotate_back(grad_in, cos_t, sin_t):
    half_dim = HEAD_DIM // 2
    scaled = grad_in * sin_t
    turned = jnp.concatenate([scaled[..., half_dim:], -scaled[..., :half_dim]], axis=-1)
    return grad_in * cos_t + turned


RELAY_A = tuple(8 * z + 2 for z in (3, 2, 1)) + tuple(8 * z + 6 for z in (1, 0))
RELAY_B = tuple(8 * z + 4 for z in (3, 2, 1)) + tuple(8 * z + 6 for z in (3, 2))
N_RELAY = 5


def far_blocks():
    out = []
    for k in range(N_RELAY):
        for core in range(2):
            out.append((RELAY_A[k] + core, 2 + core, k))
            out.append((RELAY_B[k] + core, 4 + core, k))
    return out


def near_blocks():
    return [8 * z + c for z in (3, 2, 1) for c in range(2)] + [2, 3, 4, 5, 1]


def enter_all(me):
    barrier = pltpu.get_barrier_semaphore()

    def tell(off, carry):
        pl.semaphore_signal(barrier, inc=1, device_id=(lax.rem(me + off, N_DEV),), device_id_type=MESH)
        return carry

    lax.fori_loop(1, N_DEV, tell, 0)
    pl.semaphore_wait(barrier, N_DEV - 1)


def small_gather_kernel(src, dst, send_sem, recv_sem, own_sem):
    me = lax.axis_index("fsdp")
    enter_all(me)

    def copy(off):
        return pltpu.make_async_remote_copy(
            src_ref=src, dst_ref=dst.at[me], send_sem=send_sem.at[off], recv_sem=recv_sem.at[off],
            device_id=(lax.rem(me + off, N_DEV),), device_id_type=MESH)

    def start(off, carry):
        copy(off).start()
        return carry

    def finish(off, carry):
        copy(off).wait()
        return carry

    lax.fori_loop(1, N_DEV, start, 0)
    own = pltpu.make_async_copy(src, dst.at[me], own_sem)
    own.start()
    lax.fori_loop(1, N_DEV, finish, 0)
    own.wait()


def small_gather(block):
    return pl.pallas_call(
        small_gather_kernel,
        out_shape=jax.ShapeDtypeStruct((N_DEV,) + block.shape, block.dtype),
        in_specs=[pl.BlockSpec(memory_space=pltpu.VMEM)],
        out_specs=pl.BlockSpec(memory_space=pltpu.VMEM),
        scratch_shapes=[pltpu.SemaphoreType.DMA((N_DEV,)), pltpu.SemaphoreType.DMA((N_DEV,)), pltpu.SemaphoreType.DMA],
        compiler_params=pltpu.CompilerParams(collective_id=1, has_side_effects=True),
        name="small_gather",
    )(block)


def cold_copy(me, off, src, dst, rows, send_sem, recv_sem):
    other = lax.rem(me + off, N_DEV)
    return pltpu.make_async_remote_copy(
        src_ref=src.at[pl.ds(pl.multiple_of(other * rows, rows), rows)],
        dst_ref=dst.at[pl.ds(pl.multiple_of(me * rows, rows), rows)],
        send_sem=send_sem.at[off], recv_sem=recv_sem.at[off],
        device_id=(other,), device_id_type=MESH)


def relay_ids(me, k):
    core = lax.rem(me, 2)
    is_a = me < 4
    return jnp.where(is_a, RELAY_A[k], RELAY_B[k]) + core


def lookup_kernel(hot_send, cold_send, hot_recv, cold_recv, relay, hs_sem, hr_sem, rr_sem, fs_sem, cs_sem, cr_sem, own_sem):
    me = lax.axis_index("fsdp")
    enter_all(me)

    def hot_block(dev):
        return hot_send.at[pl.ds(dev * HOT_CAP, HOT_CAP)]

    def out_copies():
        copies = []
        near = near_blocks()
        far = far_blocks()
        order = []
        while near or far:
            if far:
                order.extend(far[:4])
                far = far[4:]
            if near:
                order.extend(near[:2])
                near = near[2:]
        for item in order:
            if isinstance(item, tuple):
                dev, via, k = item
                copies.append(pltpu.make_async_remote_copy(
                    src_ref=hot_block(dev), dst_ref=relay.at[k], send_sem=hs_sem.at[dev], recv_sem=rr_sem.at[k],
                    device_id=(via,), device_id_type=MESH))
            else:
                copies.append(pltpu.make_async_remote_copy(
                    src_ref=hot_block(item), dst_ref=hot_recv, send_sem=hs_sem.at[item], recv_sem=hr_sem,
                    device_id=(item,), device_id_type=MESH))
        return copies

    @pl.when(me == 0)
    def _():
        for copy in out_copies():
            copy.start()

    def start(off, carry):
        cold_copy(me, off, cold_send, cold_recv, COLD_CAP, cs_sem, cr_sem).start()
        return carry

    lax.fori_loop(1, N_DEV, start, 0)
    own_rows = pl.ds(pl.multiple_of(me * COLD_CAP, COLD_CAP), COLD_CAP)
    own_cold = pltpu.make_async_copy(cold_send.at[own_rows], cold_recv.at[own_rows], own_sem.at[0])
    own_cold.start()
    own_hot = pltpu.make_async_copy(hot_block(0), hot_recv, own_sem.at[1])

    @pl.when(me == 0)
    def _():
        own_hot.start()

    @pl.when((me >= 2) & (me < 6))
    def _():
        def onward(k):
            return pltpu.make_async_remote_copy(
                src_ref=relay.at[k], dst_ref=hot_recv, send_sem=fs_sem.at[k], recv_sem=hr_sem,
                device_id=(relay_ids(me, k),), device_id_type=MESH)

        for k in range(N_RELAY):
            pltpu.make_async_copy(relay.at[k], relay.at[k], rr_sem.at[k]).wait()
            onward(k).start()
        for k in range(N_RELAY):
            onward(k).wait_send()

    def finish(off, carry):
        cold_copy(me, off, cold_send, cold_recv, COLD_CAP, cs_sem, cr_sem).wait()
        return carry

    lax.fori_loop(1, N_DEV, finish, 0)
    own_cold.wait()

    @pl.when(me == 0)
    def _():
        own_hot.wait()
        for copy in out_copies():
            copy.wait_send()

    @pl.when(me != 0)
    def _():
        pltpu.make_async_copy(hot_recv, hot_recv, hr_sem).wait()


def lookup_exchange(hot_send, cold_send):
    width = hot_send.shape[1]
    dma = pltpu.SemaphoreType.DMA
    return pl.pallas_call(
        lookup_kernel,
        out_shape=(jax.ShapeDtypeStruct((HOT_CAP, width), jnp.bfloat16),
                   jax.ShapeDtypeStruct((N_DEV * COLD_CAP, width), jnp.bfloat16)),
        in_specs=[pl.BlockSpec(memory_space=pl.ANY)] * 2,
        out_specs=(pl.BlockSpec(memory_space=pl.ANY),) * 2,
        scratch_shapes=[pltpu.VMEM((N_RELAY, HOT_CAP, width), jnp.bfloat16),
                        dma((N_DEV,)), dma, dma((N_RELAY,)), dma((N_RELAY,)), dma((N_DEV,)), dma((N_DEV,)), dma((2,))],
        compiler_params=pltpu.CompilerParams(collective_id=2, has_side_effects=True),
        cost_estimate=pl.CostEstimate(flops=60_000_000_000, bytes_accessed=30_000_000, transcendentals=0),
        name="lookup_exchange",
    )(hot_send, cold_send)


def return_kernel(hot_send, cold_send, vec_send, hot_recv, cold_recv, vec_recv, relay,
                  hs_sem, hr_sem, rr_sem, fs_sem, cs_sem, cr_sem, vs_sem, vr_sem, own_sem):
    me = lax.axis_index("fsdp")
    enter_all(me)

    def hot_block(dev):
        return hot_recv.at[pl.ds(pl.multiple_of(dev * HOT_CAP, HOT_CAP), HOT_CAP)]

    def direct():
        return pltpu.make_async_remote_copy(
            src_ref=hot_send, dst_ref=hot_block(me), send_sem=hs_sem, recv_sem=hr_sem.at[me],
            device_id=(0,), device_id_type=MESH)

    def to_relay(via, k):
        return pltpu.make_async_remote_copy(
            src_ref=hot_send, dst_ref=relay.at[k], send_sem=hs_sem, recv_sem=rr_sem.at[k],
            device_id=(via,), device_id_type=MESH)

    far = far_blocks()
    is_near = functools.reduce(lambda a, b: a | b, [me == dev for dev in near_blocks()])

    @pl.when(is_near)
    def _():
        direct().start()

    for dev, via, k in far:
        @pl.when(me == dev)
        def _(via=via, k=k):
            to_relay(via, k).start()

    def vec_copy(off):
        other = lax.rem(me + off, N_DEV)
        return pltpu.make_async_remote_copy(
            src_ref=vec_send.at[other], dst_ref=vec_recv.at[me], send_sem=vs_sem.at[off], recv_sem=vr_sem.at[off],
            device_id=(other,), device_id_type=MESH)

    def start(off, carry):
        cold_copy(me, off, cold_send, cold_recv, COLD_CAP, cs_sem, cr_sem).start()
        vec_copy(off).start()
        return carry

    lax.fori_loop(1, N_DEV, start, 0)
    own_rows = pl.ds(pl.multiple_of(me * COLD_CAP, COLD_CAP), COLD_CAP)
    own_cold = pltpu.make_async_copy(cold_send.at[own_rows], cold_recv.at[own_rows], own_sem.at[0])
    own_cold.start()
    own_vec = pltpu.make_async_copy(vec_send.at[me], vec_recv.at[me], own_sem.at[2])
    own_vec.start()
    own_hot = pltpu.make_async_copy(hot_send, hot_block(0), own_sem.at[1])

    @pl.when(me == 0)
    def _():
        own_hot.start()

    @pl.when((me >= 2) & (me < 6))
    def _():
        def onward(k):
            src = relay_ids(me, k)
            return pltpu.make_async_remote_copy(
                src_ref=relay.at[k], dst_ref=hot_block(src), send_sem=fs_sem.at[k], recv_sem=hr_sem.at[src],
                device_id=(0,), device_id_type=MESH)

        for k in reversed(range(N_RELAY)):
            pltpu.make_async_copy(relay.at[k], relay.at[k], rr_sem.at[k]).wait()
            onward(k).start()
        for k in range(N_RELAY):
            onward(k).wait_send()

    @pl.when(is_near)
    def _():
        direct().wait_send()

    for dev, via, k in far:
        @pl.when(me == dev)
        def _(via=via, k=k):
            to_relay(via, k).wait_send()

    def finish(off, carry):
        cold_copy(me, off, cold_send, cold_recv, COLD_CAP, cs_sem, cr_sem).wait()
        vec_copy(off).wait()
        return carry

    lax.fori_loop(1, N_DEV, finish, 0)
    own_cold.wait()
    own_vec.wait()

    @pl.when(me == 0)
    def _():
        own_hot.wait()

        def arrived(dev, carry):
            pltpu.make_async_copy(hot_block(dev), hot_block(dev), hr_sem.at[dev]).wait()
            return carry

        lax.fori_loop(1, N_DEV, arrived, 0)


def return_exchange(hot_send, cold_send, vec_send):
    width = hot_send.shape[1]
    dma = pltpu.SemaphoreType.DMA
    return pl.pallas_call(
        return_kernel,
        out_shape=(jax.ShapeDtypeStruct((N_DEV * HOT_CAP, width), jnp.bfloat16),
                   jax.ShapeDtypeStruct((N_DEV * COLD_CAP, width), jnp.bfloat16),
                   jax.ShapeDtypeStruct(vec_send.shape, jnp.float32)),
        in_specs=[pl.BlockSpec(memory_space=pl.ANY)] * 3,
        out_specs=(pl.BlockSpec(memory_space=pl.ANY),) * 3,
        scratch_shapes=[pltpu.VMEM((N_RELAY, HOT_CAP, width), jnp.bfloat16),
                        dma, dma((N_DEV,)), dma((N_RELAY,)), dma((N_RELAY,)), dma((N_DEV,)), dma((N_DEV,)),
                        dma((N_DEV,)), dma((N_DEV,)), dma((3,))],
        compiler_params=pltpu.CompilerParams(collective_id=3, has_side_effects=True),
        cost_estimate=pl.CostEstimate(flops=60_000_000_000, bytes_accessed=30_000_000, transcendentals=0),
        name="return_exchange",
    )(hot_send, cold_send, vec_send)


GRAD_TILE = 512


def weight_grad_kernel(hidden_ref, attn_ref, g_ref, out_ref):
    step = pl.program_id(0)
    dims = (((0,), (0,)), ((), ()))

    @pl.when(step < QKV // GRAD_TILE)
    def _():
        out_ref[...] = lax.dot_general(hidden_ref[...], g_ref[...], dims, preferred_element_type=jnp.float32)

    @pl.when(step >= QKV // GRAD_TILE)
    def _():
        out_ref[...] = lax.dot_general(attn_ref[...], g_ref[...], dims, preferred_element_type=jnp.float32)


def weight_grads(hidden, attn_b, grads):
    tokens, width = hidden.shape
    return pl.pallas_call(
        weight_grad_kernel,
        grid=(WCOLS // GRAD_TILE,),
        out_shape=jax.ShapeDtypeStruct((width, WCOLS), jnp.float32),
        in_specs=[pl.BlockSpec((tokens, width), lambda j: (0, 0)),
                  pl.BlockSpec((tokens, width), lambda j: (0, 0)),
                  pl.BlockSpec((tokens, GRAD_TILE), lambda j: (0, j))],
        out_specs=pl.BlockSpec((width, GRAD_TILE), lambda j: (0, j)),
        compiler_params=pltpu.CompilerParams(vmem_limit_bytes=40 * 1024 * 1024),
        cost_estimate=pl.CostEstimate(flops=2 * tokens * width * WCOLS, bytes_accessed=width * WCOLS * 4, transcendentals=0),
        name="weight_grads",
    )(hidden, attn_b, grads)


def block_fwd_bwd(x_rows, grad_out, gain_vec, w_all, b_qkv):
    seq_len, model_width = x_rows.shape
    w_qkv = w_all[:, :QKV]
    w_out = w_all[:, QKV:]
    n_heads, kv_heads = 16, 2
    q_group = n_heads // kv_heads
    q_width = n_heads * HEAD_DIM
    kv_width = kv_heads * HEAD_DIM
    score_scale = HEAD_DIM ** -0.5
    cos_t, sin_t = rope_tables(seq_len)
    x_full = x_rows.astype(jnp.float32)
    inv_rms = lax.rsqrt(jnp.mean(x_full * x_full, axis=-1, keepdims=True) + NORM_EPS)
    x_norm = x_full * inv_rms
    gain_f = gain_vec.astype(jnp.float32)
    hidden = (x_norm * gain_f).astype(jnp.bfloat16)
    lin = jnp.dot(hidden, w_qkv, preferred_element_type=jnp.float32) + b_qkv.astype(jnp.float32)
    q_lin = lin[:, :q_width]
    k_lin = lin[:, q_width:q_width + kv_width]
    v_lin = lin[:, q_width + kv_width:]
    q_rot = rotate(q_lin.reshape(seq_len, n_heads, HEAD_DIM), cos_t, sin_t).astype(jnp.bfloat16)
    q_rot = q_rot.reshape(seq_len, kv_heads, q_group, HEAD_DIM)
    k_rot = rotate(k_lin.reshape(seq_len, kv_heads, HEAD_DIM), cos_t, sin_t).astype(jnp.bfloat16)
    v_val = v_lin.astype(jnp.bfloat16).reshape(seq_len, kv_heads, HEAD_DIM)
    scores = jnp.einsum("qkgd,skd->kgqs", q_rot, k_rot, preferred_element_type=jnp.float32) * score_scale
    causal = jnp.arange(seq_len)[:, None] >= jnp.arange(seq_len)[None, :]
    scores = jnp.where(causal, scores, MASK_VALUE)
    prob_f = jax.nn.softmax(scores, axis=-1)
    prob_b = prob_f.astype(jnp.bfloat16)
    attn_out = jnp.einsum("kgqs,skd->qkgd", prob_b, v_val, preferred_element_type=jnp.float32)
    attn_b = attn_out.astype(jnp.bfloat16).reshape(seq_len, q_width)
    proj_out = jnp.dot(attn_b, w_out, preferred_element_type=jnp.float32)
    block_out = (x_full + proj_out).astype(jnp.bfloat16)

    d_attn = jnp.einsum("lo,io->li", grad_out, w_out, preferred_element_type=jnp.float32)
    d_attn = d_attn.astype(jnp.bfloat16).reshape(seq_len, kv_heads, q_group, HEAD_DIM)
    d_probs = jnp.einsum("qkgd,skd->kgqs", d_attn, v_val, preferred_element_type=jnp.float32)
    d_val = jnp.einsum("kgqs,qkgd->skd", prob_b, d_attn, preferred_element_type=jnp.float32)
    d_scores = prob_f * (d_probs - jnp.sum(d_probs * prob_f, axis=-1, keepdims=True))
    d_scores = (d_scores * score_scale).astype(jnp.bfloat16)
    d_qrot = jnp.einsum("kgqs,skd->qkgd", d_scores, k_rot, preferred_element_type=jnp.float32)
    d_krot = jnp.einsum("kgqs,qkgd->skd", d_scores, q_rot, preferred_element_type=jnp.float32)
    d_query = rotate_back(d_qrot.reshape(seq_len, n_heads, HEAD_DIM), cos_t, sin_t).reshape(seq_len, q_width)
    d_key = rotate_back(d_krot, cos_t, sin_t).reshape(seq_len, kv_width)
    d_value = d_val.reshape(seq_len, kv_width)
    d_lin = jnp.concatenate([d_query, d_key, d_value], axis=1)
    grad_b = jnp.sum(d_lin, axis=0)
    d_lin_b = d_lin.astype(jnp.bfloat16)
    grad_w = weight_grads(hidden, attn_b, jnp.concatenate([d_lin_b, grad_out], axis=1))
    d_hidden = jnp.einsum("lo,io->li", d_lin_b, w_qkv, preferred_element_type=jnp.float32)
    grad_gain = jnp.sum(d_hidden * x_norm, axis=0)
    d_norm = d_hidden * gain_f
    d_x = grad_out.astype(jnp.float32) + inv_rms * (d_norm - x_norm * jnp.mean(d_norm * x_norm, axis=-1, keepdims=True))
    return block_out, d_x, grad_w, grad_gain, grad_b


def solution(mesh):
    row_spec = P("fsdp", None)
    vec_spec = P("fsdp")
    act_spec = P("fsdp", None, None)
    weight_specs = (vec_spec, row_spec, vec_spec, row_spec, vec_spec, row_spec, vec_spec, row_spec)
    in_specs = (row_spec, act_spec, row_spec) + weight_specs
    out_specs = (act_spec, row_spec) + weight_specs

    def device_step(tok_ids, grad_out, table_part, gain_part, wq_part, bq_part, wk_part, bk_part, wv_part, bv_part, wo_part):
        rows_dev, model_width = table_part.shape
        seq_len = tok_ids.shape[1]
        me = lax.axis_index("fsdp")
        first_row = me * rows_dev
        w_all = lax.all_gather(jnp.concatenate([wq_part, wk_part, wv_part, wo_part], axis=1), "fsdp", axis=0, tiled=True)

        vec_part = jnp.concatenate([gain_part, bq_part, bk_part, bv_part]).astype(jnp.float32)
        block = jnp.concatenate([tok_ids.reshape(-1).astype(jnp.float32), jnp.pad(vec_part, (0, 1024 - 256 - 144))])
        gathered = small_gather(block.reshape(8, 128)).reshape(N_DEV, 1024)
        all_ids = gathered[:, :seq_len].astype(jnp.int32)
        vecs = gathered[:, seq_len:seq_len + 144].astype(jnp.bfloat16)
        gain_full = vecs[:, :64].reshape(-1)
        b_qkv = jnp.concatenate([vecs[:, 64:128].reshape(-1), vecs[:, 128:136].reshape(-1), vecs[:, 136:144].reshape(-1)])

        owner = all_ids // rows_dev
        before = (jnp.arange(seq_len)[:, None] < jnp.arange(seq_len)[None, :]).astype(jnp.bfloat16)
        counts = jnp.sum((owner[:, :, None] == jnp.arange(N_DEV)).astype(jnp.int32), axis=1)
        overflow = (jnp.max(counts[:, 0]) > HOT_CAP) | (jnp.max(counts[:, 1:]) > COLD_CAP)

        def slot_rows(mask, values, cap):
            rank = jnp.dot(mask.astype(jnp.bfloat16), before, preferred_element_type=jnp.float32).astype(jnp.int32)
            hit = mask[:, None, :] & (rank[:, None, :] == jnp.arange(cap)[None, :, None])
            return jnp.sum(jnp.where(hit, values[:, None, :] + 1, 0), axis=2).reshape(-1) - 1

        hot_rows = slot_rows(owner == 0, all_ids, HOT_CAP)
        cold_rows = slot_rows((owner == me) & (owner > 0), all_ids - first_row, COLD_CAP)
        hot_send = jnp.take(table_part, jnp.maximum(hot_rows, 0), axis=0)
        cold_send = jnp.take(table_part, jnp.maximum(cold_rows, 0), axis=0)
        hot_recv, cold_recv = lookup_exchange(hot_send, cold_send)

        my_ids = tok_ids.reshape(-1)
        my_owner = my_ids // rows_dev
        same = (my_owner[:, None] == my_owner[None, :]) & (jnp.arange(seq_len)[None, :] < jnp.arange(seq_len)[:, None])
        my_rank = jnp.sum(same.astype(jnp.int32), axis=1)
        hot_slot = jnp.where(my_owner == 0, my_rank, -1)
        cold_slot = jnp.where(my_owner > 0, my_owner * COLD_CAP + my_rank, -1)
        hot_pick = (hot_slot[:, None] == jnp.arange(HOT_CAP)[None, :]).astype(jnp.bfloat16)
        cold_pick = (cold_slot[:, None] == jnp.arange(N_DEV * COLD_CAP)[None, :]).astype(jnp.bfloat16)

        def rows_fast():
            picked = jnp.dot(hot_pick, hot_recv, preferred_element_type=jnp.float32)
            picked = picked + jnp.dot(cold_pick, cold_recv, preferred_element_type=jnp.float32)
            return picked.astype(jnp.bfloat16)

        def rows_dense():
            local_idx = all_ids - first_row
            is_owned = (local_idx >= 0) & (local_idx < rows_dev)
            looked = jnp.take(table_part, jnp.where(is_owned, local_idx, 0), axis=0)
            looked = jnp.where(is_owned[..., None], looked, jnp.zeros((), jnp.bfloat16))
            return lax.psum_scatter(looked, "fsdp", scatter_dimension=0)

        x_rows = lax.cond(overflow, rows_dense, rows_fast)
        g_rows = grad_out.reshape(seq_len, model_width)
        block_out, d_x, grad_w, grad_gain, grad_b = block_fwd_bwd(x_rows, g_rows, gain_full, w_all, b_qkv)
        w_red = lax.psum_scatter(grad_w, "fsdp", scatter_dimension=0, tiled=True)

        dx_b = d_x.astype(jnp.bfloat16)
        tdims = (((0,), (0,)), ((), ()))
        hot_back = lax.dot_general(hot_pick, dx_b, tdims, preferred_element_type=jnp.float32).astype(jnp.bfloat16)
        cold_back = lax.dot_general(cold_pick, dx_b, tdims, preferred_element_type=jnp.float32).astype(jnp.bfloat16)
        vec_grad = jnp.concatenate(
            [grad_gain.reshape(N_DEV, 64), grad_b[:2048].reshape(N_DEV, 64), grad_b[2048:2304].reshape(N_DEV, 8),
             grad_b[2304:].reshape(N_DEV, 8), jnp.zeros((N_DEV, 1024 - 144), jnp.float32)], axis=1)
        hot_sum, cold_sum, vec_sum = return_exchange(hot_back, cold_back, vec_grad.reshape(N_DEV, 8, 128))

        def table_fast():
            hot_idx = jnp.where((me == 0) & (hot_rows >= 0), hot_rows, rows_dev)
            cold_idx = jnp.where(cold_rows >= 0, cold_rows, rows_dev)
            total = jnp.zeros((rows_dev, model_width), jnp.float32)
            total = total.at[hot_idx].add(hot_sum.astype(jnp.float32), mode="drop")
            total = total.at[cold_idx].add(cold_sum.astype(jnp.float32), mode="drop")
            return total.astype(jnp.bfloat16)

        def table_dense():
            local_idx = all_ids - first_row
            is_owned = (local_idx >= 0) & (local_idx < rows_dev)
            all_dx = lax.all_gather(d_x, "fsdp")
            seg_idx = jnp.where(is_owned, local_idx, rows_dev)
            total = jax.ops.segment_sum(all_dx.reshape(-1, model_width), seg_idx.reshape(-1), num_segments=rows_dev)
            return total.astype(jnp.bfloat16)

        grad_table = lax.cond(overflow, table_dense, table_fast)
        v_red = jnp.sum(vec_sum.reshape(N_DEV, 1024), axis=0)
        return (block_out[None], grad_table, v_red[:64], w_red[:, :2048], v_red[64:128], w_red[:, 2048:2304],
                v_red[128:136], w_red[:, 2304:2560], v_red[136:144], w_red[:, 2560:])

    return jax.shard_map(device_step, mesh=mesh, in_specs=in_specs, out_specs=out_specs, check_vma=False)
```

time: 1740 us -> 1140 us (0.66)
  waiting for transfers between devices: 1250 us -> 463 us
  Pallas kernels: 0 us -> 298 us
  blocking collectives: 144 us -> 0 us
  other arithmetic: 177 us -> 195 us
    reduce_scatter x5 -> x1, waiting for transfers between devices: 788 us -> 334 us  [device_step(): w_red = lax.psum_scatter(grad_w, 'fsdp', scatter_dimension=0, tiled=True)]
    all_gather x5 -> x1, waiting for transfers between devices: 455 us -> 128 us  [device_step(): lax.all_gather(jnp.concatenate([wq_part, wk_part, wv_part, wo_part], axis...]
    pallas_call x0 -> x4, Pallas kernels: none -> 298 us  [the longest x1 150 us: return_exchange(): pl.pallas_call(return_kernel, out_shape=(jax.ShapeDtypeStruct((N_DEV * HO...]
    unnamed x2 -> x0, blocking collectives: 101 us -> none
    all_gather x1 -> x0, blocking collectives: 43.5 us -> none  [device_step(): all_ids = lax.all_gather(tok_ids, 'fsdp')]
    dot_general x18 -> x15, matrix products: 61.4 us -> 55.1 us  [the longest x1 8.66 us: block_fwd_bwd(): jnp.einsum('kgqs,skd->qkgd', d_scores, k_rot, preferred_element_type=jnp....]
    gather x1 -> x2, local copies, waits for them, and re-layouts: 70.4 us -> 65.2 us  [the longest x1 51.6 us: device_step(): hot_send = jnp.take(table_part, jnp.maximum(hot_rows, 0), axis=0)]
    scatter-add x1 -> x2, other arithmetic: 117 us -> 121 us  [the longest x1 88.5 us: table_fast(): total = total.at[hot_idx].add(hot_sum.astype(jnp.float32), mode='drop')]
  transfers between devices with their start and end apart: 10 -> 2, of which waited for: 9 -> 2; matrix products, arithmetic and copies ran while one was open for 17% -> 1% of each run, Pallas kernels for 0% -> 0%
where the time goes in v1:
time: 1140 us; the launch traced here: 1130 us
  waiting for transfers between devices  463 us (41%)
  Pallas kernels  298 us (26%)
  other arithmetic  195 us (17%)
  local copies, waits for them, and re-layouts  95.9 us (8%)
  matrix products  60.5 us (5%)
  between operations  17.9 us (2%)
    reduce_scatter x1, waiting for transfers between devices, device_step(): w_red = lax.psum_scatter(grad_w, 'fsdp', scatter_dimension=0, tiled=True)  334 us
    pallas_call x1, Pallas kernels, return_exchange(): pl.pallas_call(return_kernel, out_shape=(jax.ShapeDtypeStruct((N_DEV * HO...  150 us
    all_gather x1, waiting for transfers between devices, device_step(): lax.all_gather(jnp.concatenate([wq_part, wk_part, wv_part, wo_part], axis...  128 us
    pallas_call x1, Pallas kernels, lookup_exchange(): pl.pallas_call(lookup_kernel, out_shape=(jax.ShapeDtypeStruct((HOT_CAP, w...  121 us
    scatter-add x1, other arithmetic, table_fast(): total = total.at[hot_idx].add(hot_sum.astype(jnp.float32), mode='drop')  88.5 us
    gather x1, local copies, waits for them, and re-layouts, device_step(): hot_send = jnp.take(table_part, jnp.maximum(hot_rows, 0), axis=0)  51.6 us
    scatter-add x1, other arithmetic, table_fast(): total = total.at[cold_idx].add(cold_sum.astype(jnp.float32), mode='drop')  33 us
  transfers between devices with their start and end apart: 2, of which 2 were waited for; matrix products, arithmetic and copies ran while one was open for 1% of the time, Pallas kernels for 0%

profile of v1, /device:TPU:0, one launch (start us, length us, event | category | flops | bytes accessed | tf_op | source)
XLA Modules:
  0.0 1132.5 jit_solution(13238282158573230132)
XLA Ops:
  10.2 12.6 %small_gather.1 = f32[32,8,128]{2,1,0:T(8,128)} custom-call(f32[8,128]{1,0:T(8,128)} %maximum_bitcast_fusion.src), custom_call_target="tpu_custom_call" | custom-call | tf_op jit(solution)/shard_map/small_gather/pallas_call | solution.py:97
  31.8 51.6 %gather_fusion.1 = bf16[5632,2048]{1,0:T(8,128)(2,1)} fusion(bf16[4748,2048]{1,0:T(8,128)(2,1)} %param.17, s32[6144]{0:T(1024)S(1)} %pad_clamp_fusion), kind=kCustom, calls=%fused_computation.1 | custom fusion | bytes 46159872 | tf_op jit(solution)/shard_map/jit(_take)/gather | solution.py:458
  83.4 13.6 %gather_fusion.2 = bf16[512,2048]{1,0:T(8,128)(2,1)S(1)} fusion(bf16[4748,2048]{1,0:T(8,128)(2,1)} %param.17, s32[1024]{0:T(1024)S(1)} %pad_clamp_fusion.1), kind=kCustom, calls=%fused_computation.2 | custom fusion | bytes 4196352 | tf_op jit(solution)/shard_map/jit(_take)/gather | solution.py:459
  97.2 21.1 %broadcast_select_fusion.hot_send = bf16[5632,2048]{1,0:T(8,128)(2,1)} fusion(bf16[5632,2048]{1,0:T(8,128)(2,1)} %gather_fusion.1, pred[5632]{0:T(1024)(128)(4,1)S(1)} %maximum_compare_fusion), kind=kLoop, calls=%fused_computation.31 | loop fusion | flops 11534336 | bytes 46142976 | tf_op jit(solution)/shard_map/jit(_take)/select_n | solution.py:458
  119.9 120.6 %lookup_exchange.1 = (bf16[176,2048]{1,0:T(8,128)(2,1)S(1)}, bf16[512,2048]{1,0:T(8,128)(2,1)}) custom-call(bf16[5632,2048]{1,0:T(8,128)(2,1)} %broadcast_select_fusion.hot_send, bf16[512,2048]{1,0:T(8,128)(2,1)} %broadcast_select_fusion.1.cold_send), custom_call_target="tpu_custom_call" | custom-call | flops 60000002048 | bytes 30000000 | tf_op jit(solution)/shard_map/lookup_exchange/pallas_call | solution.py:207
  249.0 128.5 %all-gather.6.cloned.1.call-done = bf16[2048,4608]{1,0:T(8,128)(2,1)} async-done(((bf16[64,4608]{1,0:T(8,128)(2,1)}), bf16[2048,4608]{1,0:T(8,128)(2,1)}) %all-gather.6.cloned.1.call-update) | async-done | bytes 18874384 | tf_op jit(solution)/shard_map/all_gather | solution.py:436
  377.4 5.8 fusion.24
  385.7 2.9 copy.126
  391.6 5.4 fusion.99
  396.9 3.8 convolution_convert_fusion.2
  400.7 5.9 fusion.34
  410.9 8.4 broadcast_multiply_fusion.1
  419.2 8.7 fusion.47
  433.6 3.5 copy.105
  451.3 6.3 multiply_reduce_fusion.2
  466.3 150.1 %return_exchange.1 = (bf16[5632,2048]{1,0:T(8,128)(2,1)}, bf16[512,2048]{1,0:T(8,128)(2,1)}, f32[32,8,128]{2,1,0:T(8,128)}) custom-call(bf16[176,2048]{1,0:T(8,128)(2,1)} %convolution_convert_fusion.1.hot_send, bf16[512,2048]{1,0:T(8,128)(2,1)} %convolution_convert_fusion.cold_send, f32[32,8,128]{2,1,0:T(8,128)} %bitcast.164), custom_call_target="tpu_custom_call" | custom-call | flops 60000002048 | bytes 30000000 | tf_op jit(solution)/shard_map/return_exchange/pallas_call | solution.py:320
  616.4 142.8 %conditional.8 = (bf16[4748,2048]{1,0:T(8,128)(2,1)}) conditional(s32[]{:T(128)} %convert_element_type.137, (s32[]{:T(128)}, s32[5632]{0:T(1024)S(1)}, bf16[5632,2048]{1,0:T(8,128)(2,1)}, s32[512]{0:T(512)S(1)}, bf16[512,2048]{1,0:T(8,128)(2,1)}) %tuple.81, (s32[]{:T(128)}, s32[32,256]{1,0:T(8,128)S(1)}, f32[256,2048]{1,0:T(8,128)}) %tuple.79), branch_computations={%region_17.20_spmd, %region_20.22_spmd} | conditional | flops 34926080 | bytes 304988736
  616.5 88.5 %scatter_custom_fusion = f32[4748,2048]{1,0:T(8,128)} fusion(s32[5632]{0:T(1024)S(1)} %compare_select_fusion.1, bf16[5632,2048]{1,0:T(8,128)(2,1)} %get-tuple-element.51, f32[]{:T(128)} %constant.61.clone), kind=kCustom, calls=%fused_computation.18 | custom fusion | flops 23068672 | bytes 61964292 | tf_op jit(solution)/shard_map/cond/branch_0_fun/scatter-add | solution.py:501
  705.0 33.0 %scatter_custom_fusion.1 = f32[4748,2048]{1,0:T(8,128)} fusion(f32[4748,2048]{1,0:T(8,128)} %scatter_custom_fusion, s32[512]{0:T(512)S(1)} %compare_select_fusion.2, bf16[512,2048]{1,0:T(8,128)(2,1)} %get-tuple-element.53), kind=kCustom, calls=%fused_computation.21 | custom fusion | flops 2097152 | bytes 40992768 | tf_op jit(solution)/shard_map/cond/branch_0_fun/scatter-add | solution.py:502
  737.9 21.1 %convert_element_type.103 = bf16[4748,2048]{1,0:T(8,128)(2,1)} convert(f32[4748,2048]{1,0:T(8,128)} %scatter_custom_fusion.1) | non-fusion elementwise | flops 9723904 | bytes 58343424 | tf_op jit(solution)/shard_map/cond/branch_0_fun/convert_element_type | solution.py:503
  759.3 3.1 reduce-scatter.5.cloned.1.call-start
  763.6 14.4 %weight_grads.1 = f32[2048,4608]{1,0:T(8,128)} custom-call(bf16[256,2048]{1,0:T(8,128)(2,1)S(1)} %copy-done.1, bf16[256,2048]{1,0:T(8,128)(2,1)S(1)} %copy-done.2, bf16[256,4608]{1,0:T(8,128)(2,1)S(1)} %pad_maximum_fusion.1.g_ref), custom_call_target="tpu_custom_call" | custom-call | flops 4831838208 | bytes 37748736 | tf_op jit(solution)/shard_map/weight_grads/pallas_call | solution.py:354
  780.1 6.7 fusion.37
  786.8 334.0 %reduce-scatter.5.cloned.1.call-done = f32[64,4608]{1,0:T(8,128)} async-done(((f32[2048,4608]{1,0:T(8,128)}), f32[64,4608]{1,0:T(8,128)}) %reduce-scatter.5.cloned.1.call-update) | async-done | bytes 1179664 | tf_op jit(solution)/shard_map/reduce_scatter | solution.py:486
  (177 shorter events, 67.3 us)
Async XLA Ops:
  28.7 68.4 %copy-start.34 = (s32[256]{0:T(256)}, s32[256]{0:T(256)S(1)}, u32[]{:S(2)}) copy-start(s32[256]{0:T(256)S(1)} %get-tuple-element.123) | copy-start | bytes 3076
  97.1 21.3 %copy-start.30 = (s32[512]{0:T(512)}, s32[512]{0:T(512)S(1)}, u32[]{:S(2)}) copy-start(s32[512]{0:T(512)S(1)} %sub.71) | copy-start | bytes 6148
  119.9 120.6 %copy-start.21 = (s32[32,256]{1,0:T(8,128)S(1)}, s32[32,256]{1,0:T(8,128)}, u32[]{:S(2)}) copy-start(s32[32,256]{1,0:T(8,128)} %slice_convert_fusion.1) | copy-start | bytes 98308
  240.5 2.6 copy-start.28
  240.5 4.9 copy-start.15
  243.0 214.6 %copy-start.4 = (f32[256,2048]{1,0:T(8,128)}, f32[256,2048]{1,0:T(8,128)S(1)}, u32[]{:S(2)}) copy-start(f32[256,2048]{1,0:T(8,128)S(1)} %get-tuple-element.76) | copy-start | bytes 6291460
  243.1 134.4 %all-gather.6.cloned.1.call-start = ((), (), s32[]{:S(2)}) async-start(), calls=%async_computation.4 | async-start | bytes 19464192 | tf_op jit(solution)/shard_map/all_gather | solution.py:436
  248.9 134.3 %copy-start = (bf16[256,2048]{1,0:T(8,128)(2,1)}, bf16[256,2048]{1,0:T(8,128)(2,1)S(1)}, u32[]{:S(2)}) copy-start(bf16[256,2048]{1,0:T(8,128)(2,1)S(1)} %multiply_convert_fusion.hidden_ref) | copy-start | bytes 3145732
  391.5 5.4 copy-start.18
  391.5 5.4 copy-start.23
  396.9 3.8 copy-start.9
  400.7 5.9 copy-start.36
  400.7 5.9 copy-start.37
  410.9 8.4 copy-start.26
  429.0 22.1 %copy-start.11 = (f32[256,256]{1,0:T(8,128)}, f32[256,256]{1,0:T(8,128)S(1)}, u32[]{:S(2)}) copy-start(f32[256,256]{1,0:T(8,128)S(1)} %copy.132) | copy-start | bytes 786436
  431.8 5.3 copy-start.20
  444.5 2.9 copy-start.19
  451.2 6.4 copy-start.8
  462.0 2.7 copy-start.10
  466.3 150.1 %copy-start.22 = (s32[32,256]{1,0:T(8,128)S(1)}, s32[32,256]{1,0:T(8,128)}, u32[]{:S(2)}) copy-start(s32[32,256]{1,0:T(8,128)} %slice_convert_fusion.1) | copy-start | bytes 98308
  466.3 150.1 %copy-start.25 = (s32[5632]{0:T(1024)S(1)}, s32[5632]{0:T(1024)}, u32[]{:S(2)}) copy-start(s32[5632]{0:T(1024)} %copy-done.24) | copy-start | bytes 67588
  466.3 150.1 %copy-start.31 = (s32[512]{0:T(512)S(1)}, s32[512]{0:T(512)}, u32[]{:S(2)}) copy-start(s32[512]{0:T(512)} %copy-done.30) | copy-start | bytes 6148
  616.4 146.0 %copy-start.1 = (bf16[256,2048]{1,0:T(8,128)(2,1)S(1)}, bf16[256,2048]{1,0:T(8,128)(2,1)}, u32[]{:S(2)}) copy-start(bf16[256,2048]{1,0:T(8,128)(2,1)} %copy-done) | copy-start | bytes 3145732
  759.3 361.6 %reduce-scatter.5.cloned.1.call-start = ((), (), s32[]{:S(2)}) async-start(), calls=%async_computation.5 | async-start | bytes 38928384 | tf_op jit(solution)/shard_map/reduce_scatter | solution.py:486
  (16 other events, 25.5 us)
Sparse Core Ops, SparseCore 1:
  247.0 130.4 all-gather.5
  778.1 342.7 reduce-scatter.4
